TPU v7x, 32 devices: a whole 2x2x4 slice. The times are simulated.
32 devices in a mesh: cells: 8 (over z, x), genes: 4 (over y, core).
Axes of the slice: x: 2, y: 2, z: 4, core: 2. Of those that a mesh axis runs over, the one named last changes fastest.
Arguments:
- expression: float32 [2048, 8192], P('cells', 'genes'), may hold values from 0.1 to 3000, as said below
- donor_label: int32 [2048], P('cells'), may hold values from 0 to 255
- live_count: int32 [8], P('cells'), may hold values from 16 to 256, as said below
- genotypes: bfloat16 [4, 8, 256, 4096], P('genes', 'cells'), may hold values from 0 to 2
- covariates: float32 [256, 2], replicated, may hold values from -4 to 4
- donor_cells: int32 [256], replicated, may hold values from 200 to 4999
- win_start: int32 [4, 2048], P('genes', 'cells'), may hold values from 0 to 2048
- win_len: int32 [4, 2048], P('genes', 'cells'), may hold values from 512 to 2048, as said below
Outputs:
- correlation: float32 [4, 2048, 4096], P('genes', 'cells')
- zscore_out: float32 [4, 2048, 256], P('genes', 'cells')
Inputs may be any that keep to these rules, and one draw needn't show every extreme that they name: `live_count`: some index of cells has all 256 slots used. win_len[b0, k] is 2048 wherever k is a multiple of 256, so win_start + win_len <= 4096 throughout. `expression`: positive counts.
All inputs are finite; a program needn't handle non-finite values.
Results may differ from a plain program's by a relative error of at most 0.0003.
Values sent between devices are 32-bit elements; how exact they have to be, the bound alone decides.
A program may use at most 64 MiB of HBM per device.

v0:
```python
import jax
import jax.numpy as jnp
from jax import lax
from jax.sharding import PartitionSpec as P

HIGHEST = lax.Precision.HIGHEST
epsilon = 1e-06
cpm_scale = 10000.0


def design_matrix(covariates, donor_cells):
    log_cells = jnp.log(donor_cells.astype(jnp.float32) / 1000.0)
    ones_col = jnp.ones((covariates.shape[0], 1), jnp.float32)
    return jnp.concatenate([ones_col, log_cells[:, None], covariates], axis=1)


def invert(gram_matrix):
    width = gram_matrix.shape[0]
    augmented = jnp.concatenate([gram_matrix, jnp.eye(width, dtype=jnp.float32)], axis=1)
    for pivot in range(width):
        pivot_row = augmented[pivot] / augmented[pivot, pivot]
        augmented = augmented - augmented[:, pivot][:, None] * pivot_row[None, :]
        augmented = augmented.at[pivot].set(pivot_row)
    return augmented[:, width:]


def residualize_rows(level_rows, design, gram_inv):
    projected = jnp.dot(level_rows, design, precision=HIGHEST, preferred_element_type=jnp.float32)
    coeffs = jnp.dot(projected, gram_inv, precision=HIGHEST, preferred_element_type=jnp.float32)
    return level_rows - jnp.dot(
        coeffs, design.T, precision=HIGHEST, preferred_element_type=jnp.float32
    )


def body(
    expression, donor_label, live_count, genotypes, covariates, donor_cells, win_start, win_len
):
    donors = covariates.shape[0]
    capacity, local_genes = expression.shape
    cells_count = lax.axis_size("cells")
    block_genes = local_genes // cells_count
    design = design_matrix(covariates, donor_cells)
    gram_inv = invert(
        jnp.dot(design.T, design, precision=HIGHEST, preferred_element_type=jnp.float32)
    )
    donor_ids = jnp.arange(donors, dtype=jnp.int32)
    block_rows = min(128, capacity)
    block_count = (live_count[0] + block_rows - 1) // block_rows

    def onehot_of(labels, usable):
        return ((labels[None, :] == donor_ids[:, None]) & usable[None, :]).astype(jnp.float32)

    def local_block(turn_id):
        offset = turn_id * block_rows
        cell_rows = lax.dynamic_slice_in_dim(expression, offset, block_rows, 0)
        labels = lax.dynamic_slice_in_dim(donor_label, offset, block_rows, 0)
        usable = offset + jnp.arange(block_rows, dtype=jnp.int32) < live_count[0]
        return (cell_rows, onehot_of(labels, usable))

    def gene_major(turn_id, running):
        cell_rows, onehot = local_block(turn_id)
        return running + lax.dot_general(
            cell_rows,
            onehot,
            (((0,), (1,)), ((), ())),
            precision=HIGHEST,
            preferred_element_type=jnp.float32,
        )

    partial_value = lax.fori_loop(
        0, block_count, gene_major, jnp.zeros((local_genes, donors), jnp.float32)
    )
    totals = lax.psum(jnp.sum(partial_value, axis=0), ("cells", "genes"))
    pieces = lax.all_to_all(partial_value, "cells", split_axis=0, concat_axis=0, tiled=True)
    sums_rows = jnp.sum(pieces.reshape(cells_count, block_genes, donors), axis=0)
    level_rows = jnp.log1p(cpm_scale * sums_rows / (totals[None, :] + 1.0))
    level_rows = residualize_rows(level_rows, design, gram_inv)
    zscore_rows = level_rows * lax.rsqrt(
        jnp.mean(level_rows * level_rows, axis=1, keepdims=True) + epsilon
    )
    dosage = genotypes[0, 0].astype(jnp.float32)
    coef_x = jnp.dot(
        gram_inv,
        jnp.dot(design.T, dosage, precision=HIGHEST, preferred_element_type=jnp.float32),
        precision=HIGHEST,
        preferred_element_type=jnp.float32,
    )
    dosage_res = dosage - jnp.dot(
        design, coef_x, precision=HIGHEST, preferred_element_type=jnp.float32
    )
    dosage_z = dosage_res * lax.rsqrt(
        jnp.mean(dosage_res * dosage_res, axis=0, keepdims=True) + epsilon
    )
    correlation = (
        jnp.dot(zscore_rows, dosage_z, precision=HIGHEST, preferred_element_type=jnp.float32)
        / donors
    )
    variant = jnp.arange(dosage.shape[1], dtype=jnp.int32)
    first = win_start[0]
    inside = (variant[None, :] >= first[:, None]) & (
        variant[None, :] < (first + win_len[0])[:, None]
    )
    correlation = jnp.where(inside, correlation, jnp.float32(0.0))
    return (correlation[None], zscore_rows[None])


def solution(mesh):
    placed = (
        P("cells", "genes"),
        P("cells"),
        P("cells"),
        P("genes", "cells", None, None),
        P(),
        P(),
        P("genes", "cells"),
        P("genes", "cells"),
    )
    return jax.shard_map(
        body,
        mesh=mesh,
        in_specs=placed,
        out_specs=(P("genes", "cells", None), P("genes", "cells", None)),
        check_vma=False,
    )
```

profile of v0, /device:TPU:0, one launch (start us, length us, event | category | flops | bytes accessed | tf_op | source)
XLA Modules:
  0.0 109.5 jit_solution(6040645947162707037)
XLA Ops:
  1.3 1.5 %broadcast_in_dim.16 = f32[2048,256]{1,0:T(8,128)} broadcast(f32[]{:T(128)} %constant.148.clone.1), dimensions={} | broadcast | bytes 2097156 | tf_op jit(solution)/shard_map/broadcast_in_dim | solution.py:71
  2.8 11.4 %while.15 = (s32[]{:T(128)}, f32[2048,256]{1,0:T(8,128)}, s32[]{:T(128)}, f32[256,2048]{1,0:T(8,128)}, s32[256]{0:T(256)}, /*index=5*/s32[1]{0:T(128)}, s32[]{:T(128)}, s32[]{:T(128)}, s32[]{:T(128)}, s32[]{:T(128)}) while((s32[]{:T(128)}, f32[2048,256]{1,0:T(8,128)}, s32[]{:T(128)}, f32[256,2048]{1,0:T(8,128)}, s32[256]{0:T(256)}, ...), condition=%wide.region_1.0_spmd.clone, body=%wide.region_0.0_spmd.clone.sunk | while | flops 805896448 | bytes 5244843 | solution.py:70
  2.8 0.8 dynamic_slice.13
  3.5 0.7 add_compare_fusion.2
  4.2 4.3 %convolution_add_fusion.2 = f32[2048,256]{1,0:T(8,128)} fusion(f32[2048,256]{1,0:T(8,128)} %get-tuple-element.175, f32[256,2048]{1,0:T(8,128)} %get-tuple-element.187, s32[]{:T(128)S(6)} %select_n.20, s32[128]{0:T(128)S(1)} %dynamic_slice.13, pred[128]{0:T(512)(128)(4,1)S(1)} %add_compare_fusion.2), kind=kOutput, calls=%fused_computation.1.clone.1 | convolution fusion | flops 805896192 | bytes 5243524 | tf_op jit(solution)/shard_map/while/body/dot_general | solution.py:62
  8.4 0.8 dynamic_slice.13
  9.2 0.7 add_compare_fusion.2
  9.8 4.3 %convolution_add_fusion.2 = f32[2048,256]{1,0:T(8,128)} fusion(f32[2048,256]{1,0:T(8,128)} %get-tuple-element.175, f32[256,2048]{1,0:T(8,128)} %get-tuple-element.187, s32[]{:T(128)S(6)} %select_n.20, s32[128]{0:T(128)S(1)} %dynamic_slice.13, pred[128]{0:T(512)(128)(4,1)S(1)} %add_compare_fusion.2), kind=kOutput, calls=%fused_computation.1.clone.1 | convolution fusion | flops 805896192 | bytes 5243524 | tf_op jit(solution)/shard_map/while/body/dot_general | solution.py:62
  14.1 0.0 copy-start.3
  14.1 0.0 copy-start
  14.1 0.0 copy-start.1
  14.1 0.0 copy-start.2
  14.1 4.5 %all-to-all-start = ((f32[8,256,256]{2,1,0:T(8,128)}), f32[8,256,256]{2,1,0:T(8,128)S(1)}, u32[]{:S(2)}, u32[]{:S(2)}) async-start(f32[8,256,256]{2,1,0:T(8,128)} %bitcast.3), calls=%async_computation | async-start | bytes 4194304 | tf_op jit(solution)/shard_map/all_to_all | solution.py:74
  18.6 0.0 copy-done.3
  18.6 0.0 copy-done
  18.7 0.2 fusion.24
  18.9 0.5 slice.101
  19.4 0.1 slice_reduce_fusion.3
  19.5 0.1 pad_maximum_fusion.1
  19.6 0.7 fusion.32
  20.2 0.7 slice_divide_fusion.3
  20.9 1.9 %reduce_sum.37 = f32[256]{0:T(256)S(1)} reduce(f32[2048,256]{1,0:T(8,128)} %get-tuple-element.88, f32[]{:T(128)} %constant.148.clone.1), dimensions={0}, to_apply=%region_3.0 | reduce | flops 524032 | bytes 2098180 | tf_op jit(solution)/shard_map/reduce_sum | solution.py:73
  22.8 0.1 multiply_subtract_fusion.3
  22.9 0.6 slice.104
  23.5 0.2 slice_reduce_fusion.2
  23.6 0.7 fusion.31
  24.3 0.7 slice_divide_fusion.2
  25.0 0.1 multiply_subtract_fusion.2
  25.1 0.6 slice.107
  25.7 0.2 slice_reduce_fusion.1
  25.8 0.7 fusion.30
  26.5 0.7 slice_divide_fusion.1
  27.2 0.1 multiply_subtract_fusion.1
  27.3 0.6 slice.110
  27.8 0.0 copy-done.1
  27.9 0.0 copy-done.2
  27.9 0.2 slice_reduce_fusion
  28.0 0.7 fusion.29
  28.7 0.7 slice_divide_fusion
  29.4 0.1 multiply_subtract_fusion
  29.5 58.6 %psum.7 = f32[256]{0:T(256)S(1)} all-reduce(f32[256]{0:T(256)S(1)} %reduce_sum.37), channel_id=1, replica_groups=mesh['cells'=8,'genes'=4] {'cells','genes'}, use_global_device_ids=true, to_apply=%region_4.5 | all-reduce | flops 256 | bytes 2048 | tf_op jit(solution)/shard_map/psum | solution.py:73
  88.1 2.5 %fusion.12 = f32[4,4096]{1,0:T(4,128)S(1)} fusion(bf16[1,1,256,4096]{3,2,1,0:T(8,128)(2,1)} %param.21, f32[256,2]{0,1:T(2,128)S(1)} %copy-done, f32[256,1]{0,1:T(1,128)S(1)} %bitcast.34, f32[4]{0:T(128)S(1)} %pad.10.clone), kind=kOutput, calls=%fused_computation.18 | convolution fusion | flops 50333696 | bytes 2165776 | tf_op jit(solution)/shard_map/dot_general | solution.py:84
  90.6 0.3 fusion.19
  91.0 6.8 %multiply_reduce_fusion = (f32[4096]{0:T(1024)S(1)}, f32[256,4096]{1,0:T(8,128)}) fusion(f32[4,4096]{1,0:T(4,128)S(1)} %fusion.19, f32[256,2]{0,1:T(2,128)S(1)} %copy-done, f32[256,1]{0,1:T(1,128)S(1)} %bitcast.35, f32[4]{0:T(128)S(1)} %pad.10.clone, bf16[1,1,256,4096]{3,2,1,0:T(8,128)(2,1)} %param.21), kind=kOutput, calls=%fused_computation.14 | convolution fusion | flops 54523904 | bytes 6376464 | tf_op jit(solution)/shard_map/dot_general | solution.py:88
  97.7 0.0 all-to-all-done
  97.8 0.1 reduce_sum.36
  97.9 0.1 copy.12
  98.0 0.4 fusion.17
  98.4 0.3 fusion.21
  98.7 0.6 multiply_reduce_fusion.1
  99.3 0.8 copy.13
  100.2 9.3 %fusion.9 = f32[1,256,4096]{2,1,0:T(8,128)} fusion(f32[256,4096]{1,0:T(8,128)} %get-tuple-element.123, f32[4096]{0:T(1024)S(1)} %add_rsqrt_fusion, s32[256]{0:T(256)S(1)} %add.72, s32[256]{0:T(256)S(1)} %bitcast.39, f32[256,256]{0,1:T(8,128)S(1)} %get-tuple-element.125, f32[256]{0:T(256)S(1)} %add_rsqrt_fusion.1), kind=kOutput, calls=%fused_computation.12 | convolution fusion | flops 3227582464 | bytes 8670208 | tf_op jit(solution)/shard_map/dot_general | solution.py:95
  (12 shorter events, 0.2 us)
Async XLA Ops:
  14.1 4.5 %copy-start.3 = (s32[256]{0:T(256)S(1)}, s32[256]{0:T(256)}, u32[]{:S(2)}) copy-start(s32[256]{0:T(256)} %param.23) | copy-start | bytes 3076
  14.1 4.5 %copy-start = (f32[256,2]{0,1:T(2,128)S(1)}, f32[256,2]{0,1:T(2,128)}, u32[]{:S(2)}) copy-start(f32[256,2]{0,1:T(2,128)} %param.22) | copy-start | bytes 6148
  14.1 13.7 %copy-start.1 = (s32[1,256]{1,0:T(1,128)S(1)}, s32[1,256]{1,0:T(1,128)}, u32[]{:S(2)}) copy-start(s32[1,256]{1,0:T(1,128)} %param.24) | copy-start | bytes 3076
  14.1 13.7 %copy-start.2 = (s32[1,256]{1,0:T(1,128)S(1)}, s32[1,256]{1,0:T(1,128)}, u32[]{:S(2)}) copy-start(s32[1,256]{1,0:T(1,128)} %param.25) | copy-start | bytes 3076
  14.1 83.6 %all-to-all-start = ((f32[8,256,256]{2,1,0:T(8,128)}), f32[8,256,256]{2,1,0:T(8,128)S(1)}, u32[]{:S(2)}, u32[]{:S(2)}) async-start(f32[8,256,256]{2,1,0:T(8,128)} %bitcast.3), calls=%async_computation | async-start | bytes 4194304 | tf_op jit(solution)/shard_map/all_to_all | solution.py:74
where the time goes:
time: 110 us; the launch traced here: 109 us
  blocking collectives  58.6 us (53%)
  matrix products  28.9 us (26%)
  other arithmetic  8.95 us (8%)
  local copies, waits for them, and re-layouts  7.03 us (6%)
  starting transfers between devices  4.47 us (4%)
  between operations  1.47 us (1%)
    psum x1, blocking collectives, body(): totals = lax.psum(jnp.sum(partial_value, axis=0), ('cells', 'genes'))  58.6 us
    dot_general x1, matrix products, body(): jnp.dot(zscore_rows, dosage_z, precision=HIGHEST, preferred_element_type=...  9.29 us
    dot_general x2, matrix products, gene_major(): lax.dot_general(cell_rows, onehot, (((0,), (1,)), ((), ())), precision=HI...  8.55 us
    dot_general x1, matrix products, body(): jnp.dot(design, coef_x, precision=HIGHEST, preferred_element_type=jnp.flo...  6.76 us
    all_to_all x1, starting transfers between devices, body(): lax.all_to_all(partial_value, 'cells', split_axis=0, concat_axis=0, tiled...  4.47 us
    div x4, other arithmetic, invert(): pivot_row = augmented[pivot] / augmented[pivot, pivot]  2.61 us
    mul x4, other arithmetic, invert(): augmented = augmented - augmented[:, pivot][:, None] * pivot_row[None, :]  2.6 us
    dot_general x1, matrix products, body(): jnp.dot(design.T, dosage, precision=HIGHEST, preferred_element_type=jnp.f...  2.55 us
  transfers between devices with their start and end apart: 1, of which 0 were waited for; matrix products, arithmetic and copies ran while one was open for 19% of the time, Pallas kernels for 0%

commit v1 on v0

--- a/solution.py
+++ b/solution.py
@@ -70,7 +70,7 @@
     partial_value = lax.fori_loop(
         0, block_count, gene_major, jnp.zeros((local_genes, donors), jnp.float32)
     )
-    totals = lax.psum(jnp.sum(partial_value, axis=0), ("cells", "genes"))
+    totals = lax.psum(lax.psum(jnp.sum(partial_value, axis=0), "genes"), "cells")
     pieces = lax.all_to_all(partial_value, "cells", split_axis=0, concat_axis=0, tiled=True)
     sums_rows = jnp.sum(pieces.reshape(cells_count, block_genes, donors), axis=0)
     level_rows = jnp.log1p(cpm_scale * sums_rows / (totals[None, :] + 1.0))

time: 110 us -> 96.5 us (0.88)
  the two profiles are of different devices: /device:TPU:0 before, /device:TPU:12 now
where the time goes in v1:
time: 96.5 us; the launch traced here: 96 us
  blocking collectives  45.5 us (47%)
  matrix products  28.9 us (30%)
  other arithmetic  8.96 us (9%)
  local copies, waits for them, and re-layouts  7.03 us (7%)
  starting transfers between devices  4.11 us (4%)
  between operations  1.46 us (2%)
    psum x1, blocking collectives, body(): lax.psum(lax.psum(jnp.sum(partial_value, axis=0), 'genes'), 'cells')  39.5 us
    dot_general x1, matrix products, body(): jnp.dot(zscore_rows, dosage_z, precision=HIGHEST, preferred_element_type=...  9.3 us
    dot_general x2, matrix products, gene_major(): lax.dot_general(cell_rows, onehot, (((0,), (1,)), ((), ())), precision=HI...  8.55 us
    dot_general x1, matrix products, body(): jnp.dot(design, coef_x, precision=HIGHEST, preferred_element_type=jnp.flo...  6.76 us
    psum x1, blocking collectives, body(): lax.psum(jnp.sum(partial_value, axis=0), 'genes')  5.95 us
    all_to_all x1, starting transfers between devices, body(): lax.all_to_all(partial_value, 'cells', split_axis=0, concat_axis=0, tiled...  4.11 us
    div x4, other arithmetic, invert(): pivot_row = augmented[pivot] / augmented[pivot, pivot]  2.61 us
    mul x4, other arithmetic, invert(): augmented = augmented - augmented[:, pivot][:, None] * pivot_row[None, :]  2.6 us
  transfers between devices with their start and end apart: 1, of which 0 were waited for; matrix products, arithmetic and copies ran while one was open for 21% of the time, Pallas kernels for 0%

profile of v1, /device:TPU:12, one launch (start us, length us, event | category | flops | bytes accessed | tf_op | source)
XLA Modules:
  0.0 96.0 jit_solution(6833687939694063432)
XLA Ops:
  1.3 1.5 %broadcast_in_dim.16 = f32[2048,256]{1,0:T(8,128)} broadcast(f32[]{:T(128)} %constant.148.clone.1), dimensions={} | broadcast | bytes 2097156 | tf_op jit(solution)/shard_map/broadcast_in_dim | solution.py:71
  2.8 11.4 %while.15 = (s32[]{:T(128)}, f32[2048,256]{1,0:T(8,128)}, s32[]{:T(128)}, f32[256,2048]{1,0:T(8,128)}, s32[256]{0:T(256)}, /*index=5*/s32[1]{0:T(128)}, s32[]{:T(128)}, s32[]{:T(128)}, s32[]{:T(128)}, s32[]{:T(128)}) while((s32[]{:T(128)}, f32[2048,256]{1,0:T(8,128)}, s32[]{:T(128)}, f32[256,2048]{1,0:T(8,128)}, s32[256]{0:T(256)}, ...), condition=%wide.region_1.0_spmd.clone, body=%wide.region_0.0_spmd.clone.sunk | while | flops 805896448 | bytes 5244843 | solution.py:70
  2.8 0.8 dynamic_slice.13
  3.5 0.7 add_compare_fusion.2
  4.2 4.3 %convolution_add_fusion.2 = f32[2048,256]{1,0:T(8,128)} fusion(f32[2048,256]{1,0:T(8,128)} %get-tuple-element.175, f32[256,2048]{1,0:T(8,128)} %get-tuple-element.187, s32[]{:T(128)S(6)} %select_n.20, s32[128]{0:T(128)S(1)} %dynamic_slice.13, pred[128]{0:T(512)(128)(4,1)S(1)} %add_compare_fusion.2), kind=kOutput, calls=%fused_computation.1.clone.1 | convolution fusion | flops 805896192 | bytes 5243524 | tf_op jit(solution)/shard_map/while/body/dot_general | solution.py:62
  8.4 0.8 dynamic_slice.13
  9.2 0.7 add_compare_fusion.2
  9.8 4.3 %convolution_add_fusion.2 = f32[2048,256]{1,0:T(8,128)} fusion(f32[2048,256]{1,0:T(8,128)} %get-tuple-element.175, f32[256,2048]{1,0:T(8,128)} %get-tuple-element.187, s32[]{:T(128)S(6)} %select_n.20, s32[128]{0:T(128)S(1)} %dynamic_slice.13, pred[128]{0:T(512)(128)(4,1)S(1)} %add_compare_fusion.2), kind=kOutput, calls=%fused_computation.1.clone.1 | convolution fusion | flops 805896192 | bytes 5243524 | tf_op jit(solution)/shard_map/while/body/dot_general | solution.py:62
  14.1 0.0 copy-start.3
  14.1 0.0 copy-start
  14.1 0.0 copy-start.1
  14.1 0.0 copy-start.2
  14.1 4.1 %all-to-all-start = ((f32[8,256,256]{2,1,0:T(8,128)}), f32[8,256,256]{2,1,0:T(8,128)S(1)}, u32[]{:S(2)}, u32[]{:S(2)}) async-start(f32[8,256,256]{2,1,0:T(8,128)} %bitcast.3), calls=%async_computation | async-start | bytes 4194304 | tf_op jit(solution)/shard_map/all_to_all | solution.py:74
  18.2 0.0 copy-done.3
  18.3 0.0 copy-done
  18.3 0.2 fusion.24
  18.5 0.5 slice.101
  19.0 0.1 slice_reduce_fusion.3
  19.1 0.1 pad_maximum_fusion.1
  19.2 0.7 fusion.32
  19.9 0.7 slice_divide_fusion.3
  20.5 1.9 %reduce_sum.37 = f32[256]{0:T(256)S(1)} reduce(f32[2048,256]{1,0:T(8,128)} %get-tuple-element.88, f32[]{:T(128)} %constant.148.clone.1), dimensions={0}, to_apply=%region_3.0 | reduce | flops 524032 | bytes 2098180 | tf_op jit(solution)/shard_map/reduce_sum | solution.py:73
  22.4 0.1 multiply_subtract_fusion.3
  22.5 0.6 slice.104
  23.1 0.2 slice_reduce_fusion.2
  23.3 0.7 fusion.31
  23.9 0.7 slice_divide_fusion.2
  24.6 0.1 multiply_subtract_fusion.2
  24.7 0.6 slice.107
  25.3 0.2 slice_reduce_fusion.1
  25.5 0.7 fusion.30
  26.1 0.7 slice_divide_fusion.1
  26.8 0.1 multiply_subtract_fusion.1
  26.9 0.6 slice.110
  27.5 0.0 copy-done.1
  27.5 0.0 copy-done.2
  27.5 0.2 slice_reduce_fusion
  27.7 0.7 fusion.29
  28.3 0.7 slice_divide_fusion
  29.0 0.1 multiply_subtract_fusion
  29.1 6.0 %psum.14 = f32[256]{0:T(256)S(1)} all-reduce(f32[256]{0:T(256)S(1)} %reduce_sum.37), channel_id=1, replica_groups=mesh['cells'=8,'genes'=4] {'genes'}, use_global_device_ids=true, to_apply=%region_4.5 | all-reduce | flops 256 | bytes 2048 | tf_op jit(solution)/shard_map/psum | solution.py:73
  35.0 39.5 %psum.15 = f32[256]{0:T(256)S(1)} all-reduce(f32[256]{0:T(256)S(1)} %psum.14), channel_id=1, replica_groups=mesh['cells'=8,'genes'=4] {'cells'}, use_global_device_ids=true, to_apply=%region_5.6 | all-reduce | flops 256 | bytes 2048 | tf_op jit(solution)/shard_map/psum | solution.py:73
  74.6 2.5 %fusion.12 = f32[4,4096]{1,0:T(4,128)S(1)} fusion(bf16[1,1,256,4096]{3,2,1,0:T(8,128)(2,1)} %param.21, f32[256,2]{0,1:T(2,128)S(1)} %copy-done, f32[256,1]{0,1:T(1,128)S(1)} %bitcast.34, f32[4]{0:T(128)S(1)} %pad.10.clone), kind=kOutput, calls=%fused_computation.18 | convolution fusion | flops 50333696 | bytes 2165776 | tf_op jit(solution)/shard_map/dot_general | solution.py:84
  77.1 0.3 fusion.19
  77.5 6.8 %multiply_reduce_fusion = (f32[4096]{0:T(1024)S(1)}, f32[256,4096]{1,0:T(8,128)}) fusion(f32[4,4096]{1,0:T(4,128)S(1)} %fusion.19, f32[256,2]{0,1:T(2,128)S(1)} %copy-done, f32[256,1]{0,1:T(1,128)S(1)} %bitcast.35, f32[4]{0:T(128)S(1)} %pad.10.clone, bf16[1,1,256,4096]{3,2,1,0:T(8,128)(2,1)} %param.21), kind=kOutput, calls=%fused_computation.14 | convolution fusion | flops 54523904 | bytes 6376464 | tf_op jit(solution)/shard_map/dot_general | solution.py:88
  84.3 0.0 all-to-all-done
  84.3 0.1 reduce_sum.36
  84.4 0.1 copy.12
  84.6 0.4 fusion.17
  84.9 0.3 fusion.21
  85.2 0.6 multiply_reduce_fusion.1
  85.8 0.8 copy.13
  86.7 9.3 %fusion.9 = f32[1,256,4096]{2,1,0:T(8,128)} fusion(f32[256,4096]{1,0:T(8,128)} %get-tuple-element.123, f32[4096]{0:T(1024)S(1)} %add_rsqrt_fusion, s32[256]{0:T(256)S(1)} %add.74, s32[256]{0:T(256)S(1)} %bitcast.39, f32[256,256]{0,1:T(8,128)S(1)} %get-tuple-element.125, f32[256]{0:T(256)S(1)} %add_rsqrt_fusion.1), kind=kOutput, calls=%fused_computation.12 | convolution fusion | flops 3227582464 | bytes 8670208 | tf_op jit(solution)/shard_map/dot_general | solution.py:95
  (12 shorter events, 0.2 us)
Async XLA Ops:
  14.1 4.1 %copy-start.3 = (s32[256]{0:T(256)S(1)}, s32[256]{0:T(256)}, u32[]{:S(2)}) copy-start(s32[256]{0:T(256)} %param.23) | copy-start | bytes 3076
  14.1 4.2 %copy-start = (f32[256,2]{0,1:T(2,128)S(1)}, f32[256,2]{0,1:T(2,128)}, u32[]{:S(2)}) copy-start(f32[256,2]{0,1:T(2,128)} %param.22) | copy-start | bytes 6148
  14.1 13.4 %copy-start.1 = (s32[1,256]{1,0:T(1,128)S(1)}, s32[1,256]{1,0:T(1,128)}, u32[]{:S(2)}) copy-start(s32[1,256]{1,0:T(1,128)} %param.24) | copy-start | bytes 3076
  14.1 13.4 %copy-start.2 = (s32[1,256]{1,0:T(1,128)S(1)}, s32[1,256]{1,0:T(1,128)}, u32[]{:S(2)}) copy-start(s32[1,256]{1,0:T(1,128)} %param.25) | copy-start | bytes 3076
  14.1 70.1 %all-to-all-start = ((f32[8,256,256]{2,1,0:T(8,128)}), f32[8,256,256]{2,1,0:T(8,128)S(1)}, u32[]{:S(2)}, u32[]{:S(2)}) async-start(f32[8,256,256]{2,1,0:T(8,128)} %bitcast.3), calls=%async_computation | async-start | bytes 4194304 | tf_op jit(solution)/shard_map/all_to_all | solution.py:74
